TPU v7x, 256 devices: a whole 4x4x8 slice. The times are simulated.
256 devices in a mesh: task: 32 (over z, y), occ: 8 (over x, core).
Axes of the slice: x: 4, y: 4, z: 8, core: 2. Of those that a mesh axis runs over, the one named last changes fastest.
Arguments:
- ao_tiles: bfloat16 [5120, 8, 32, 128], P('task'), may hold values from -6 to 6
- mo_coeffs: bfloat16 [1536, 200], P(None, 'occ'), may hold values from -0.5 to 0.5
- mu_blocks: int32 [5120], P('task'), may hold values from 0 to 191
- nu_blocks: int32 [5120], P('task'), may hold values from 0 to 47
- tile_live: int32 [5120], P('task'), may hold values 0 or 1
- batch_target: int32 [640], P('task'), may hold values from 0 to 2
- batch_count: int32 [32], P('task'), may hold values from 1 to 20
Outputs:
- half_mo: float32 [200, 200, 4096], P('occ', None, 'task')
Inputs may be any that keep to these rules, and one draw needn't show every extreme that they name: `batch_target`: the batch's kl block is the block owned by task index (own index + value) mod 32. `batch_count`: batches at or after this count in a list are not part of the work.
All inputs are finite; a program needn't handle non-finite values. No bound on the sum of `tile_live` on one device may be relied on, other than what follows from the above.
Results may differ from a plain program's by a relative error of at most 0.0029.
Values may be sent and summed in bfloat16 or wider, within the bound.
No kernel may reach another device: no remote copies, remote signals or barrier semaphores. Data moves between devices by JAX's collectives and lax.ppermute only.
A program may use at most 128 MiB of HBM per device.

v0:
```python
import functools

import jax
import jax.numpy as jnp
from jax import lax
from jax.experimental import pallas as pl
from jax.experimental.pallas import tpu as pltpu
from jax.sharding import PartitionSpec as P


SPREAD = 3
GROUP = 8
BUFFERS = 4
NU = 32
VMEM_BYTES = 46 << 20
BF16 = jnp.bfloat16
SMEM = pl.BlockSpec(memory_space=pltpu.SMEM)
VMEM = pl.BlockSpec(memory_space=pltpu.VMEM)
ANY = pl.BlockSpec(memory_space=pl.ANY)


def list_kernel(mu_ref, nu_ref, live_ref, target_ref, count_ref, out_ref, *, stride, zero_block):
    per_batch = mu_ref.shape[0] // target_ref.shape[0]
    size = 3 * stride
    for s in range(SPREAD):
        out_ref[SPREAD * size + s] = 0

    def one_batch(b, carry):
        s = target_ref[b]
        n = out_ref[SPREAD * size + s]
        for q in range(per_batch):
            g = b * per_batch + q
            out_ref[s * size + n] = g
            out_ref[s * size + stride + n] = mu_ref[g]
            out_ref[s * size + 2 * stride + n] = nu_ref[g]
            n = n + live_ref[g]
        out_ref[SPREAD * size + s] = n
        return carry

    lax.fori_loop(0, count_ref[0], one_batch, 0)
    for s in range(SPREAD):
        n = out_ref[SPREAD * size + s]
        for q in range(GROUP):
            out_ref[s * size + n + q] = 0
            out_ref[s * size + stride + n + q] = 0
            out_ref[s * size + 2 * stride + n + q] = zero_block


def expand_rows(rows_ref, padded, expand):
    padded[: rows_ref.shape[0], :] = rows_ref[...]
    chunks = rows_ref.shape[1] // 128
    left = jnp.concatenate([padded[:, c * 128 : (c + 1) * 128] for c in range(chunks)], axis=0)
    row = lax.broadcasted_iota(jnp.int32, (128, 256), 0)
    lane = lax.broadcasted_iota(jnp.int32, (128, 256), 1)
    for pair in range(8):
        select = jnp.where(row == pair * 16 + lane // 16, 1.0, 0.0).astype(BF16)
        wide = jnp.dot(left, select, preferred_element_type=jnp.float32)
        for c in range(chunks):
            for half in range(2):
                expand[c * 16 + pair * 2 + half] = wide[c * 32 : (c + 1) * 32, half * 128 : (half + 1) * 128]


def tile_copies(tiles_ref, lists, base, tile_buf, sems):
    def copy(c, q):
        slot = lists[base + c * GROUP + q]
        return pltpu.make_async_copy(tiles_ref.at[slot], tile_buf.at[c % BUFFERS, q], sems.at[c % BUFFERS, q])

    return copy


def start_tiles(copy, c, groups):
    @pl.when(c < groups)
    def _():
        for q in range(GROUP):
            copy(c, q).start()


def diagonal_mask():
    row = lax.broadcasted_iota(jnp.int32, (16, 128), 0)
    lane = lax.broadcasted_iota(jnp.int32, (16, 128), 1)
    return (lane % 16) == row


def quarter_tile(mask, expand, mu, tile, q, ids, out):
    left = jnp.concatenate(
        [jnp.where(mask, jnp.broadcast_to(expand[mu, pl.ds(i, 1), :], (16, 128)), 0.0).astype(BF16) for i in ids], axis=0
    )
    right = jnp.concatenate([tile[:, :16, :].reshape(128, 128), tile[:, 16:, :].reshape(128, 128)], axis=1)
    part = jnp.dot(left, right, preferred_element_type=jnp.float32).astype(BF16)
    for i in range(len(ids)):
        out[q * NU : q * NU + 16, i * 128 : (i + 1) * 128] = part[i * 16 : (i + 1) * 16, :128]
        out[q * NU + 16 : (q + 1) * NU, i * 128 : (i + 1) * 128] = part[i * 16 : (i + 1) * 16, 128:]


def coeff_group(coeff_ref, lists, at, all_occ):
    blocks = [coeff_ref[pl.ds(pl.multiple_of(lists[at + q] * NU, NU), NU), :] for q in range(GROUP)]
    return jnp.concatenate(blocks, axis=0).T[:all_occ]


def gather_coefficients(blocks, stacked, coeff, occ):
    ranks = len(blocks)
    nbf = stacked.shape[1]
    me = lax.axis_index("occ")
    row = lax.broadcasted_iota(jnp.int32, (32, 256), 0)
    lane = lax.broadcasted_iota(jnp.int32, (32, 256), 1)
    place = []
    for r in range(ranks):
        rank = (me + 2 * (r // 2)) % ranks
        rank = rank + (r % 2) * (1 - 2 * (rank % 2))
        place.append(jnp.where((lane == rank * occ + row) & (row < occ), 1.0, 0.0).astype(BF16))
        stacked[r * 32 : (r + 1) * 32, :] = jnp.zeros((32, nbf), BF16)
        stacked[r * 32 : r * 32 + occ, :] = blocks[r][...]
    place = jnp.concatenate(place, axis=0)
    for c in range(nbf // 256):
        coeff[c * 256 : (c + 1) * 256, :] = jnp.dot(
            stacked[:, c * 256 : (c + 1) * 256].T, place, preferred_element_type=jnp.float32
        ).astype(BF16)
    coeff[nbf:, :] = jnp.zeros((NU, 256), BF16)


def partial_kernel(lists_ref, tiles_ref, rows_ref, *refs, ids, pieces, after, assemble, direct, target, stride, all_occ):
    coeff_refs, refs = refs[: max(assemble, 1)], refs[max(assemble, 1) + after :]
    outs, refs = refs[: len(pieces) + bool(assemble)], refs[len(pieces) + bool(assemble) :]
    coeff_all, outs = (outs[0], outs[1:]) if assemble else (None, outs)
    lists, rows, padded, expand, tile_buf, quarter, acc, coeff, tile_sems, sems, *rest = refs
    kl = tile_buf.shape[-1]
    lists_in = pltpu.make_async_copy(lists_ref, lists, sems.at[0])
    lists_in.start()
    rows_in = pltpu.make_async_copy(rows_ref, rows, sems.at[1])
    rows_in.start()
    if assemble:
        *blocks, stacked = rest[: assemble + 1]
        rest = rest[assemble + 1 :]
        coeff_in = [pltpu.make_async_copy(ref, block, sems.at[2 + r]) for r, (ref, block) in enumerate(zip(coeff_refs, blocks))]
        coeff_out = pltpu.make_async_copy(coeff, coeff_all, sems.at[2])
    else:
        coeff_in = [pltpu.make_async_copy(coeff_refs[0], coeff, sems.at[2])]
    for one in coeff_in:
        one.start()
    acc[...] = jnp.zeros_like(acc)
    base = target * 3 * stride
    lists_in.wait()
    groups = (lists[3 * SPREAD * stride + target] + GROUP - 1) // GROUP
    copy = tile_copies(tiles_ref, lists, base, tile_buf, tile_sems)
    for c in range(BUFFERS - 1):
        start_tiles(copy, c, groups)
    rows_in.wait()
    expand_rows(rows, padded, expand)
    for one in coeff_in:
        one.wait()
    if assemble:
        gather_coefficients(blocks, stacked, coeff, rows.shape[0])
        coeff_out.start()
    mask = diagonal_mask()

    def take(c):
        start_tiles(copy, c + BUFFERS - 1, groups)
        for q in range(GROUP):
            copy(c, q).wait()

    def make_quarter(c):
        for q in range(GROUP):
            quarter_tile(mask, expand, lists[base + stride + c * GROUP + q], tile_buf[c % BUFFERS, q], q, ids, quarter)

    def add_group(c):
        left = coeff_group(coeff, lists, base + 2 * stride + c * GROUP, all_occ)
        acc[...] += jnp.dot(left, quarter[...], preferred_element_type=jnp.float32)

    @pl.when(groups > 0)
    def _():
        take(0)
        make_quarter(0)

    def one_group(c, carry):
        take(c + 1)
        add_group(c)
        make_quarter(c + 1)
        return carry

    lax.fori_loop(0, groups - 1, one_group, 0)

    puts = []
    at = 0
    for out, piece in zip(outs, pieces):
        for k in range(piece):
            source = acc.at[:, (at + k) * kl : (at + k + 1) * kl] if direct else rest[0].at[at + k]
            puts.append(pltpu.make_async_copy(source, out.at[k], rest[-1].at[at + k]))
        at += piece

    def finish(total):
        at = 0
        for piece in pieces:
            value = total(slice(at * kl, (at + piece) * kl))
            for k in range(piece):
                if direct:
                    acc[:, (at + k) * kl : (at + k + 1) * kl] = value[:, k * kl : (k + 1) * kl]
                else:
                    rest[0][at + k] = value[:, k * kl : (k + 1) * kl].astype(rest[0].dtype)
                puts[at + k].start()
            at += piece

    @pl.when(groups > 0)
    def _():
        left = coeff_group(coeff, lists, base + 2 * stride + (groups - 1) * GROUP, all_occ)
        finish(lambda cols: acc[:, cols] + jnp.dot(left, quarter[:, cols], preferred_element_type=jnp.float32))

    @pl.when(groups == 0)
    def _():
        finish(lambda cols: acc[:, cols])

    for put in puts:
        put.wait()
    if assemble:
        coeff_out.wait()


def cost(flops, moved):
    return pl.CostEstimate(flops=flops, bytes_accessed=moved, transcendentals=0)


def lists_of(mu_blocks, nu_blocks, tile_live, batch_target, batch_count, stride, nbf):
    return pl.pallas_call(
        functools.partial(list_kernel, stride=stride, zero_block=nbf // NU),
        out_shape=jax.ShapeDtypeStruct((3 * SPREAD * stride + SPREAD,), jnp.int32),
        in_specs=[SMEM] * 5,
        out_specs=SMEM,
        cost_estimate=cost(2_000_000_000, 10_000),
        name="lists",
    )(mu_blocks, nu_blocks, tile_live, batch_target, batch_count)


def partial_sum(lists, tiles, rows, coeff, all_occ, spans, target, stride, dtype, after=()):
    occ, nbf = rows.shape
    kl = tiles.shape[3]
    ids = [i for low, high in spans for i in range(low, high)]
    pieces = [high - low for low, high in spans]
    assemble = len(coeff) if isinstance(coeff, list) else 0
    direct = dtype == jnp.float32
    shapes = [jax.ShapeDtypeStruct((piece, all_occ, kl), dtype) for piece in pieces]
    scratch = [
        pltpu.SMEM(lists.shape, jnp.int32),
        pltpu.VMEM((occ, nbf), BF16),
        pltpu.VMEM((32, nbf), BF16),
        pltpu.VMEM((nbf // 8, 32, 128), jnp.float32),
        pltpu.VMEM((BUFFERS, GROUP, *tiles.shape[1:]), BF16),
        pltpu.VMEM((GROUP * NU, len(ids) * kl), BF16),
        pltpu.VMEM((all_occ, len(ids) * kl), jnp.float32),
        pltpu.VMEM((nbf + NU, 256), BF16),
        pltpu.SemaphoreType.DMA((BUFFERS, GROUP)),
        pltpu.SemaphoreType.DMA((2 + max(assemble, 1),)),
    ]
    if assemble:
        shapes = [jax.ShapeDtypeStruct((nbf + NU, 256), BF16)] + shapes
        scratch += [pltpu.VMEM(block.shape, BF16) for block in coeff] + [pltpu.VMEM((256, nbf), BF16)]
    if not direct:
        scratch += [pltpu.VMEM((len(ids), all_occ, kl), dtype)]
    scratch += [pltpu.SemaphoreType.DMA((len(ids),))]
    coeff = coeff if assemble else [coeff]
    return pl.pallas_call(
        functools.partial(
            partial_kernel, ids=ids, pieces=pieces, after=len(after), assemble=assemble, direct=direct, target=target, stride=stride, all_occ=all_occ
        ),
        out_shape=tuple(shapes),
        in_specs=[ANY] * (3 + len(coeff) + len(after)),
        out_specs=(ANY,) * len(shapes),
        scratch_shapes=scratch,
        compiler_params=pltpu.CompilerParams(vmem_limit_bytes=VMEM_BYTES if direct else None),
        cost_estimate=cost(6_000_000_000, 10_000_000),
        name="partial",
    )(lists, tiles, rows, *coeff, *after)


def local(ao_tiles, mo_coeffs, mu_blocks, nu_blocks, tile_live, batch_target, batch_count):
    nbf, occ = mo_coeffs.shape
    ranks = lax.axis_size("occ")
    tasks = lax.axis_size("task")
    all_occ = occ * ranks
    stride = ao_tiles.shape[0] + GROUP
    rows = mo_coeffs.T

    others = [lax.ppermute(rows, "occ", [((r + 2 * d) % ranks, r) for r in range(ranks)]) for d in range(1, ranks // 2)]
    lists = lists_of(mu_blocks, nu_blocks, tile_live, batch_target, batch_count, stride, nbf)
    others, lists = lax.optimization_barrier((others, lists))
    blocks = []
    for block in [rows] + others:
        blocks += [block, lax.ppermute(block, "occ", [(r ^ 1, r) for r in range(ranks)])]

    ring = 4
    ahead = [(t, (t + 1) % tasks) for t in range(tasks)]
    back = [(t, t // ring * ring + (t - 1) % ring) for t in range(tasks)]
    back_on = [(t // ring * ring + (t - 1) % ring, (t + 2) % tasks) for t in range(tasks)]
    wide = jnp.float32
    cut, half = 8, 19

    def part(**kwargs):
        return partial_sum(lists, ao_tiles, rows, all_occ=all_occ, stride=stride, **kwargs)

    def sent(array, route):
        return lax.ppermute(array, "task", route)

    coeff_all, two_low, two_a, two_b = part(coeff=blocks, spans=[(0, cut), (cut, half), (half, occ)], target=2, dtype=BF16)
    back_a = sent(two_a, back)
    chain = sent(two_low, ahead)
    back_b = sent(two_b, back)
    (one_high,) = part(coeff=coeff_all, spans=[(cut, occ)], target=1, dtype=BF16)
    (one_low,) = part(coeff=coeff_all, spans=[(0, cut)], target=1, dtype=BF16, after=(one_high,))
    near = sent(one_high, ahead)
    far_a = sent(back_a, back_on)
    summed = (chain.astype(wide) + one_low.astype(wide)).astype(BF16)
    last = sent(summed, ahead)
    far_b = sent(back_b, back_on)
    (out,) = part(coeff=coeff_all, spans=[(0, occ)], target=0, dtype=wide, after=(back_a,))
    added = jnp.concatenate([last.astype(wide), near[: half - cut].astype(wide) + far_a.astype(wide), near[half - cut :].astype(wide) + far_b.astype(wide)])
    return out + added


def solution(mesh):
    in_specs = (P("task", None, None, None), P(None, "occ"), P("task"), P("task"), P("task"), P("task"), P("task"))
    return jax.shard_map(local, mesh=mesh, in_specs=in_specs, out_specs=P("occ", None, "task"), check_vma=False)
```

profile of v0, /device:TPU:1, one launch (start us, length us, event | category | flops | bytes accessed | tf_op | source)
XLA Modules:
  0.0 72.3 jit_solution(9466737439539651663)
XLA Ops:
  0.0 3.2 %collective-permute-start.3 = (bf16[25,1536]{1,0:T(8,128)(2,1)}, bf16[25,1536]{1,0:T(8,128)(2,1)S(1)}, u32[]{:S(2)}, u32[]{:S(2)}) collective-permute-start(bf16[25,1536]{1,0:T(8,128)(2,1)} %bitcast.1), channel_id=1, source_target_pairs={{1,0},{0,1},{3,2},{2,3},{5,4},{4,5},{7,6},{6,7},{9,8},{8,9},{11,10... | collective-permute-start | bytes 230408 | tf_op jit(solution)/shard_map/ppermute | solution.py:286
  3.2 0.0 collective-permute-start.2
  3.2 2.0 %collective-permute-start.1 = (bf16[25,1536]{1,0:T(8,128)(2,1)}, bf16[25,1536]{1,0:T(8,128)(2,1)S(1)}, u32[]{:S(2)}, u32[]{:S(2)}) collective-permute-start(bf16[25,1536]{1,0:T(8,128)(2,1)} %bitcast.3), channel_id=1, source_target_pairs={{4,0},{5,1},{6,2},{7,3},{0,4},{1,5},{2,6},{3,7},{12,8},{13,9},{14,... | collective-permute-start | bytes 230408 | tf_op jit(solution)/shard_map/ppermute | solution.py:281
  5.2 1.2 %collective-permute-start = (bf16[25,1536]{1,0:T(8,128)(2,1)}, bf16[25,1536]{1,0:T(8,128)(2,1)S(1)}, u32[]{:S(2)}, u32[]{:S(2)}) collective-permute-start(bf16[25,1536]{1,0:T(8,128)(2,1)} %bitcast.4), channel_id=1, source_target_pairs={{2,0},{3,1},{4,2},{5,3},{6,4},{7,5},{0,6},{1,7},{10,8},{11,9},{12,... | collective-permute-start | bytes 230408 | tf_op jit(solution)/shard_map/ppermute | solution.py:281
  7.0 1.8 %lists.1.lists_ref = s32[1515]{0:T(1024)} custom-call(s32[160]{0:T(256)} %mu_ref.1, s32[160]{0:T(256)} %nu_ref.1, s32[160]{0:T(256)} %live_ref.1, s32[20]{0:T(128)} %target_ref.1, s32[1]{0:T(128)S(6)} %copy.8.count_ref), custom_call_target="tpu_custom_call" | custom-call | flops 2000000000 | bytes 10000 | tf_op jit(solution)/shard_map/lists/pallas_call | solution.py:222
  8.8 2.3 %collective-permute-done.2.refs_6_ = bf16[25,1536]{1,0:T(8,128)(2,1)S(1)} collective-permute-done((bf16[25,1536]{1,0:T(8,128)(2,1)}, bf16[25,1536]{1,0:T(8,128)(2,1)S(1)}, u32[]{:S(2)}, u32[]{:S(2)}) %collective-permute-start.2) | collective-permute-done | bytes 76832 | tf_op jit(solution)/shard_map/ppermute | solution.py:281
  11.1 0.0 copy-start.4
  11.1 0.0 collective-permute-done.1.refs_4_
  11.1 0.0 copy-start.5
  11.1 0.3 collective-permute-done.refs_2_
  11.4 0.0 copy-start.6
  11.4 1.1 %collective-permute-start.4 = (bf16[25,1536]{1,0:T(8,128)(2,1)S(1)}, bf16[25,1536]{1,0:T(8,128)(2,1)S(1)}, u32[]{:S(2)}, u32[]{:S(2)}) collective-permute-start(bf16[25,1536]{1,0:T(8,128)(2,1)S(1)} %collective-permute-done.refs_2_), channel_id=1, source_target_pairs={{1,0},{0,1},{3,2},{2,3},{5,4},{4,5},{7,6},{6,7},{9,8},{8,9},{11,10... | collective-permute-start | bytes 230408 | tf_op jit(solution)/shard_map/ppermute | solution.py:286
  12.5 0.0 collective-permute-start.5
  12.5 0.5 collective-permute-start.6
  13.0 0.0 collective-permute-done.3.refs_1_
  13.0 0.0 copy-start.3
  13.0 0.4 collective-permute-done.4.refs_3_
  13.5 0.0 copy-start.7
  13.5 0.4 collective-permute-done.5.refs_5_
  13.8 0.0 copy-start.8
  13.8 0.2 collective-permute-done.6.refs_7_
  14.0 0.0 copy-done.4
  14.0 0.0 copy-done.5
  14.0 0.0 copy-done.6
  14.0 0.0 copy-done.3
  14.0 0.1 copy-done.7
  14.1 0.4 copy-done.8
  14.5 0.0 copy-start.9
  14.5 0.6 copy-done.9
  15.1 5.5 %partial.4 = (bf16[1568,256]{1,0:T(8,128)(2,1)}, bf16[8,200,128]{2,1,0:T(8,128)(2,1)}, bf16[11,200,128]{2,1,0:T(8,128)(2,1)}, bf16[6,200,128]{2,1,0:T(8,128)(2,1)}) custom-call(s32[1515]{0:T(1024)} %lists.1.lists_ref, bf16[160,8,32,128]{3,2,1,0:T(8,128)(2,1)} %tiles_ref.7, bf16[25,1536]{1,0:T(8,128)(2,1)} %bitcast.5, bf16[25,1536]{1,0:T(8,128)(2,1)} %bitcast.6, ...), custom_call_target="tpu_custom_call" | custom-call | flops 6000000000 | bytes 10000000 | tf_op jit(solution)/shard_map/partial/pallas_call | solution.py:259
  20.6 1.6 %collective-permute-start.12 = (bf16[6,200,128]{2,1,0:T(8,128)(2,1)}, bf16[6,200,128]{2,1,0:T(8,128)(2,1)S(1)}, u32[]{:S(2)}, u32[]{:S(2)}) collective-permute-start(bf16[6,200,128]{2,1,0:T(8,128)(2,1)} %get-tuple-element.20), channel_id=1, source_target_pairs={{0,24},{8,0},{16,8},{24,16},{32,56},{40,32},{48,40},{56,48},{64,88... | collective-permute-start | bytes 921608 | tf_op jit(solution)/shard_map/ppermute | solution.py:299
  22.2 4.9 %collective-permute-start.8 = (bf16[8,200,128]{2,1,0:T(8,128)(2,1)}, bf16[8,200,128]{2,1,0:T(8,128)(2,1)S(1)}, u32[]{:S(2)}, u32[]{:S(2)}) collective-permute-start(bf16[8,200,128]{2,1,0:T(8,128)(2,1)} %get-tuple-element.19), channel_id=1, source_target_pairs={{0,8},{8,16},{16,24},{24,32},{32,40},{40,48},{48,56},{56,64},{64,7... | collective-permute-start | bytes 1228808 | tf_op jit(solution)/shard_map/ppermute | solution.py:299
  27.1 4.3 %collective-permute-start.7 = (bf16[11,200,128]{2,1,0:T(8,128)(2,1)}, bf16[11,200,128]{2,1,0:T(8,128)(2,1)S(1)}, u32[]{:S(2)}, u32[]{:S(2)}) collective-permute-start(bf16[11,200,128]{2,1,0:T(8,128)(2,1)} %get-tuple-element.18), channel_id=1, source_target_pairs={{0,24},{8,0},{16,8},{24,16},{32,56},{40,32},{48,40},{56,48},{64,88... | collective-permute-start | bytes 1689608 | tf_op jit(solution)/shard_map/ppermute | solution.py:299
  31.4 6.4 %partial.6.refs_1_ = bf16[17,200,128]{2,1,0:T(8,128)(2,1)} custom-call(s32[1515]{0:T(1024)} %lists.1.lists_ref, bf16[160,8,32,128]{3,2,1,0:T(8,128)(2,1)} %tiles_ref.7, bf16[25,1536]{1,0:T(8,128)(2,1)} %bitcast.7, bf16[1568,256]{1,0:T(8,128)(2,1)} %get-tuple-element.17.refs_0_), custom_call_target="tpu_custom_call" | custom-call | flops 6000000000 | bytes 10000000 | tf_op jit(solution)/shard_map/partial/pallas_call | solution.py:259
  37.9 0.0 copy-start
  37.9 0.0 copy-start.1
  37.9 0.0 copy-start.2
  37.9 0.1 collective-permute-start.10
  38.0 5.1 %partial.7 = bf16[8,200,128]{2,1,0:T(8,128)(2,1)} custom-call(s32[1515]{0:T(1024)} %lists.1.lists_ref, bf16[160,8,32,128]{3,2,1,0:T(8,128)(2,1)} %tiles_ref.7, bf16[25,1536]{1,0:T(8,128)(2,1)} %bitcast.8, bf16[1568,256]{1,0:T(8,128)(2,1)} %get-tuple-element.17.refs_0_, bf16[17,200,128]{2,1,0:T(8,128)(2,1)} %partial.6.refs_1_), custom_call_target="tpu_custom_call" | custom-call | flops 6000000000 | bytes 10000000 | tf_op jit(solution)/shard_map/partial/pallas_call | solution.py:259
  43.1 0.0 collective-permute-done.12
  43.1 0.1 collective-permute-start.13
  43.2 0.0 collective-permute-done.8
  43.2 1.1 %add_convert_fusion = bf16[8,200,128]{2,1,0:T(8,128)(2,1)S(1)} fusion(bf16[8,200,128]{2,1,0:T(8,128)(2,1)} %partial.7, bf16[8,200,128]{2,1,0:T(8,128)(2,1)S(1)} %collective-permute-done.8), kind=kLoop, calls=%fused_computation.2 | loop fusion | flops 819200 | bytes 1228800 | tf_op jit(solution)/shard_map/convert_element_type | solution.py:309
  44.3 0.1 collective-permute-start.9
  44.4 2.4 %collective-permute-done.7.refs_1_ = bf16[11,200,128]{2,1,0:T(8,128)(2,1)S(1)} collective-permute-done((bf16[11,200,128]{2,1,0:T(8,128)(2,1)}, bf16[11,200,128]{2,1,0:T(8,128)(2,1)S(1)}, u32[]{:S(2)}, u32[]{:S(2)}) %collective-permute-start.7) | collective-permute-done | bytes 563232 | tf_op jit(solution)/shard_map/ppermute | solution.py:299
  46.8 1.7 %collective-permute-start.11 = (bf16[11,200,128]{2,1,0:T(8,128)(2,1)S(1)}, bf16[11,200,128]{2,1,0:T(8,128)(2,1)S(1)}, u32[]{:S(2)}, u32[]{:S(2)}) collective-permute-start(bf16[11,200,128]{2,1,0:T(8,128)(2,1)S(1)} %collective-permute-done.7.refs_1_), channel_id=1, source_target_pairs={{24,16},{0,24},{8,32},{16,40},{56,48},{32,56},{40,64},{48,72},{88,... | collective-permute-start | bytes 1689608 | tf_op jit(solution)/shard_map/ppermute | solution.py:299
  48.5 0.0 copy-done
  48.5 0.0 copy-done.1
  48.5 0.0 copy-done.2
  48.5 5.0 %partial.5 = f32[25,200,128]{2,1,0:T(8,128)S(1)} custom-call(s32[1515]{0:T(1024)S(1)} %copy-done.2, bf16[160,8,32,128]{3,2,1,0:T(8,128)(2,1)} %tiles_ref.7, bf16[25,1536]{1,0:T(8,128)(2,1)S(1)} %bitcast.9, bf16[1568,256]{1,0:T(8,128)(2,1)S(1)} %copy-done.1, bf16[11,200,128]{2,1,0:T(8,128)(2,1)S(1)} %collective-permute-done.7.refs_1_), custom_call_target="tpu_custom_call" | custom-call | flops 6000000000 | bytes 10000000 | tf_op jit(solution)/shard_map/partial/pallas_call | solution.py:259
  53.4 16.7 %collective-permute-done.9 = bf16[8,200,128]{2,1,0:T(8,128)(2,1)S(1)} collective-permute-done((bf16[8,200,128]{2,1,0:T(8,128)(2,1)S(1)}, bf16[8,200,128]{2,1,0:T(8,128)(2,1)S(1)}, u32[]{:S(2)}, u32[]{:S(2)}) %collective-permute-start.9) | collective-permute-done | bytes 409632 | tf_op jit(solution)/shard_map/ppermute | solution.py:299
  70.2 0.1 convert_element_type.27
  70.2 0.0 collective-permute-done.13
  70.3 0.0 collective-permute-done.10
  70.3 0.1 convert_add_fusion.1
  70.4 0.0 collective-permute-done.11
  70.4 0.1 convert_add_fusion
  70.5 1.8 %maximum_add_fusion = f32[25,200,128]{2,1,0:T(8,128)} fusion(f32[25,200,128]{2,1,0:T(8,128)S(1)} %partial.5, f32[6,200,128]{2,1,0:T(8,128)S(1)} %convert_add_fusion.1, f32[11,200,128]{2,1,0:T(8,128)S(1)} %convert_add_fusion, f32[8,200,128]{2,1,0:T(8,128)S(1)} %convert_element_type.27), kind=kLoop, calls=%fused_computation | loop fusion | flops 1920000 | bytes 7680000 | tf_op jit(solution)/shard_map/add | solution.py:314
Async XLA Ops:
  0.0 13.0 %collective-permute-start.3 = (bf16[25,1536]{1,0:T(8,128)(2,1)}, bf16[25,1536]{1,0:T(8,128)(2,1)S(1)}, u32[]{:S(2)}, u32[]{:S(2)}) collective-permute-start(bf16[25,1536]{1,0:T(8,128)(2,1)} %bitcast.1), channel_id=1, source_target_pairs={{1,0},{0,1},{3,2},{2,3},{5,4},{4,5},{7,6},{6,7},{9,8},{8,9},{11,10... | collective-permute-start | bytes 230408 | tf_op jit(solution)/shard_map/ppermute | solution.py:286
  3.2 7.9 %collective-permute-start.2 = (bf16[25,1536]{1,0:T(8,128)(2,1)}, bf16[25,1536]{1,0:T(8,128)(2,1)S(1)}, u32[]{:S(2)}, u32[]{:S(2)}) collective-permute-start(bf16[25,1536]{1,0:T(8,128)(2,1)} %bitcast.2), channel_id=1, source_target_pairs={{6,0},{7,1},{0,2},{1,3},{2,4},{3,5},{4,6},{5,7},{14,8},{15,9},{8,1... | collective-permute-start | bytes 230408 | tf_op jit(solution)/shard_map/ppermute | solution.py:281
  3.2 7.9 %collective-permute-start.1 = (bf16[25,1536]{1,0:T(8,128)(2,1)}, bf16[25,1536]{1,0:T(8,128)(2,1)S(1)}, u32[]{:S(2)}, u32[]{:S(2)}) collective-permute-start(bf16[25,1536]{1,0:T(8,128)(2,1)} %bitcast.3), channel_id=1, source_target_pairs={{4,0},{5,1},{6,2},{7,3},{0,4},{1,5},{2,6},{3,7},{12,8},{13,9},{14,... | collective-permute-start | bytes 230408 | tf_op jit(solution)/shard_map/ppermute | solution.py:281
  5.2 6.2 %collective-permute-start = (bf16[25,1536]{1,0:T(8,128)(2,1)}, bf16[25,1536]{1,0:T(8,128)(2,1)S(1)}, u32[]{:S(2)}, u32[]{:S(2)}) collective-permute-start(bf16[25,1536]{1,0:T(8,128)(2,1)} %bitcast.4), channel_id=1, source_target_pairs={{2,0},{3,1},{4,2},{5,3},{6,4},{7,5},{0,6},{1,7},{10,8},{11,9},{12,... | collective-permute-start | bytes 230408 | tf_op jit(solution)/shard_map/ppermute | solution.py:281
  11.1 2.9 %copy-start.4 = (bf16[25,1536]{1,0:T(8,128)(2,1)}, bf16[25,1536]{1,0:T(8,128)(2,1)S(1)}, u32[]{:S(2)}) copy-start(bf16[25,1536]{1,0:T(8,128)(2,1)S(1)} %collective-permute-done.2.refs_6_) | copy-start | bytes 230404
  11.1 2.9 %copy-start.5 = (bf16[25,1536]{1,0:T(8,128)(2,1)}, bf16[25,1536]{1,0:T(8,128)(2,1)S(1)}, u32[]{:S(2)}) copy-start(bf16[25,1536]{1,0:T(8,128)(2,1)S(1)} %collective-permute-done.1.refs_4_) | copy-start | bytes 230404
  11.4 2.6 %copy-start.6 = (bf16[25,1536]{1,0:T(8,128)(2,1)}, bf16[25,1536]{1,0:T(8,128)(2,1)S(1)}, u32[]{:S(2)}) copy-start(bf16[25,1536]{1,0:T(8,128)(2,1)S(1)} %collective-permute-done.refs_2_) | copy-start | bytes 230404
  11.4 2.1 %collective-permute-start.4 = (bf16[25,1536]{1,0:T(8,128)(2,1)S(1)}, bf16[25,1536]{1,0:T(8,128)(2,1)S(1)}, u32[]{:S(2)}, u32[]{:S(2)}) collective-permute-start(bf16[25,1536]{1,0:T(8,128)(2,1)S(1)} %collective-permute-done.refs_2_), channel_id=1, source_target_pairs={{1,0},{0,1},{3,2},{2,3},{5,4},{4,5},{7,6},{6,7},{9,8},{8,9},{11,10... | collective-permute-start | bytes 230408 | tf_op jit(solution)/shard_map/ppermute | solution.py:286
  12.5 1.3 %collective-permute-start.5 = (bf16[25,1536]{1,0:T(8,128)(2,1)S(1)}, bf16[25,1536]{1,0:T(8,128)(2,1)S(1)}, u32[]{:S(2)}, u32[]{:S(2)}) collective-permute-start(bf16[25,1536]{1,0:T(8,128)(2,1)S(1)} %collective-permute-done.1.refs_4_), channel_id=1, source_target_pairs={{1,0},{0,1},{3,2},{2,3},{5,4},{4,5},{7,6},{6,7},{9,8},{8,9},{11,10... | collective-permute-start | bytes 230408 | tf_op jit(solution)/shard_map/ppermute | solution.py:286
  12.5 1.5 %collective-permute-start.6 = (bf16[25,1536]{1,0:T(8,128)(2,1)S(1)}, bf16[25,1536]{1,0:T(8,128)(2,1)S(1)}, u32[]{:S(2)}, u32[]{:S(2)}) collective-permute-start(bf16[25,1536]{1,0:T(8,128)(2,1)S(1)} %collective-permute-done.2.refs_6_), channel_id=1, source_target_pairs={{1,0},{0,1},{3,2},{2,3},{5,4},{4,5},{7,6},{6,7},{9,8},{8,9},{11,10... | collective-permute-start | bytes 230408 | tf_op jit(solution)/shard_map/ppermute | solution.py:286
  13.0 1.0 %copy-start.3 = (bf16[25,1536]{1,0:T(8,128)(2,1)}, bf16[25,1536]{1,0:T(8,128)(2,1)S(1)}, u32[]{:S(2)}) copy-start(bf16[25,1536]{1,0:T(8,128)(2,1)S(1)} %collective-permute-done.3.refs_1_) | copy-start | bytes 230404
  13.5 0.6 copy-start.7
  13.8 0.7 copy-start.8
  14.5 0.6 copy-start.9
  20.6 22.5 %collective-permute-start.12 = (bf16[6,200,128]{2,1,0:T(8,128)(2,1)}, bf16[6,200,128]{2,1,0:T(8,128)(2,1)S(1)}, u32[]{:S(2)}, u32[]{:S(2)}) collective-permute-start(bf16[6,200,128]{2,1,0:T(8,128)(2,1)} %get-tuple-element.20), channel_id=1, source_target_pairs={{0,24},{8,0},{16,8},{24,16},{32,56},{40,32},{48,40},{56,48},{64,88... | collective-permute-start | bytes 921608 | tf_op jit(solution)/shard_map/ppermute | solution.py:299
  22.2 21.0 %collective-permute-start.8 = (bf16[8,200,128]{2,1,0:T(8,128)(2,1)}, bf16[8,200,128]{2,1,0:T(8,128)(2,1)S(1)}, u32[]{:S(2)}, u32[]{:S(2)}) collective-permute-start(bf16[8,200,128]{2,1,0:T(8,128)(2,1)} %get-tuple-element.19), channel_id=1, source_target_pairs={{0,8},{8,16},{16,24},{24,32},{32,40},{40,48},{48,56},{56,64},{64,7... | collective-permute-start | bytes 1228808 | tf_op jit(solution)/shard_map/ppermute | solution.py:299
  27.1 19.7 %collective-permute-start.7 = (bf16[11,200,128]{2,1,0:T(8,128)(2,1)}, bf16[11,200,128]{2,1,0:T(8,128)(2,1)S(1)}, u32[]{:S(2)}, u32[]{:S(2)}) collective-permute-start(bf16[11,200,128]{2,1,0:T(8,128)(2,1)} %get-tuple-element.18), channel_id=1, source_target_pairs={{0,24},{8,0},{16,8},{24,16},{32,56},{40,32},{48,40},{56,48},{64,88... | collective-permute-start | bytes 1689608 | tf_op jit(solution)/shard_map/ppermute | solution.py:299
  37.9 10.6 %copy-start = (bf16[1536,25]{0,1:T(8,128)(2,1)S(1)}, bf16[1536,25]{0,1:T(8,128)(2,1)}, u32[]{:S(2)}) copy-start(bf16[1536,25]{0,1:T(8,128)(2,1)} %param.8) | copy-start | bytes 230404
  37.9 10.6 %copy-start.1 = (bf16[1568,256]{1,0:T(8,128)(2,1)S(1)}, bf16[1568,256]{1,0:T(8,128)(2,1)}, u32[]{:S(2)}) copy-start(bf16[1568,256]{1,0:T(8,128)(2,1)} %get-tuple-element.17.refs_0_) | copy-start | bytes 2408452
  37.9 10.6 %copy-start.2 = (s32[1515]{0:T(1024)S(1)}, s32[1515]{0:T(1024)}, u32[]{:S(2)}) copy-start(s32[1515]{0:T(1024)} %lists.1.lists_ref) | copy-start | bytes 18184
  37.9 32.4 %collective-permute-start.10 = (bf16[17,200,128]{2,1,0:T(8,128)(2,1)}, bf16[17,200,128]{2,1,0:T(8,128)(2,1)S(1)}, u32[]{:S(2)}, u32[]{:S(2)}) collective-permute-start(bf16[17,200,128]{2,1,0:T(8,128)(2,1)} %partial.6.refs_1_), channel_id=1, source_target_pairs={{0,8},{8,16},{16,24},{24,32},{32,40},{40,48},{48,56},{56,64},{64,7... | collective-permute-start | bytes 2611208 | tf_op jit(solution)/shard_map/ppermute | solution.py:299
  43.1 27.2 %collective-permute-start.13 = (bf16[6,200,128]{2,1,0:T(8,128)(2,1)S(1)}, bf16[6,200,128]{2,1,0:T(8,128)(2,1)S(1)}, u32[]{:S(2)}, u32[]{:S(2)}) collective-permute-start(bf16[6,200,128]{2,1,0:T(8,128)(2,1)S(1)} %collective-permute-done.12), channel_id=1, source_target_pairs={{24,16},{0,24},{8,32},{16,40},{56,48},{32,56},{40,64},{48,72},{88,... | collective-permute-start | bytes 921608 | tf_op jit(solution)/shard_map/ppermute | solution.py:299
  44.3 25.9 %collective-permute-start.9 = (bf16[8,200,128]{2,1,0:T(8,128)(2,1)S(1)}, bf16[8,200,128]{2,1,0:T(8,128)(2,1)S(1)}, u32[]{:S(2)}, u32[]{:S(2)}) collective-permute-start(bf16[8,200,128]{2,1,0:T(8,128)(2,1)S(1)} %add_convert_fusion), channel_id=1, source_target_pairs={{0,8},{8,16},{16,24},{24,32},{32,40},{40,48},{48,56},{56,64},{64,7... | collective-permute-start | bytes 1228808 | tf_op jit(solution)/shard_map/ppermute | solution.py:299
  46.8 23.6 %collective-permute-start.11 = (bf16[11,200,128]{2,1,0:T(8,128)(2,1)S(1)}, bf16[11,200,128]{2,1,0:T(8,128)(2,1)S(1)}, u32[]{:S(2)}, u32[]{:S(2)}) collective-permute-start(bf16[11,200,128]{2,1,0:T(8,128)(2,1)S(1)} %collective-permute-done.7.refs_1_), channel_id=1, source_target_pairs={{24,16},{0,24},{8,32},{16,40},{56,48},{32,56},{40,64},{48,72},{88,... | collective-permute-start | bytes 1689608 | tf_op jit(solution)/shard_map/ppermute | solution.py:299
where the time goes:
time: 72.8 us; the launch traced here: 72.3 us
  Pallas kernels  23.7 us (33%)
  waiting for transfers between devices  22.7 us (31%)
  starting transfers between devices  20.7 us (28%)
  other arithmetic  3.22 us (4%)
  local copies, waits for them, and re-layouts  1.15 us (2%)
  between operations  0.81 us (1%)
    pallas_call x4, Pallas kernels, partial_sum(): pl.pallas_call(functools.partial(partial_kernel, ids=ids, pieces=pieces,...  21.9 us
    ppermute x7, waiting for transfers between devices, sent(): return lax.ppermute(array, 'task', route)  19.2 us
    ppermute x7, starting transfers between devices, sent(): return lax.ppermute(array, 'task', route)  12.8 us
    ppermute x4, starting transfers between devices, local(): lax.ppermute(block, 'occ', [(r ^ 1, r) for r in range(ranks)])  4.85 us
    ppermute x3, starting transfers between devices, local(): lax.ppermute(rows, 'occ', [((r + 2 * d) % ranks, r) for r in range(ranks)])  3.11 us
    ppermute x3, waiting for transfers between devices, local(): lax.ppermute(rows, 'occ', [((r + 2 * d) % ranks, r) for r in range(ranks)])  2.61 us
    add x1, other arithmetic, local(): return out + added  1.83 us
    pallas_call x1, Pallas kernels, lists_of(): pl.pallas_call(functools.partial(list_kernel, stride=stride, zero_block=n...  1.8 us
  transfers between devices with their start and end apart: 14, of which 7 were waited for; matrix products, arithmetic and copies ran while one was open for 2% of the time, Pallas kernels for 25%

commit v1 on v0

--- a/solution.py
+++ b/solution.py
@@ -302,14 +302,13 @@
     back_a = sent(two_a, back)
     chain = sent(two_low, ahead)
     back_b = sent(two_b, back)
-    (one_high,) = part(coeff=coeff_all, spans=[(cut, occ)], target=1, dtype=BF16)
-    (one_low,) = part(coeff=coeff_all, spans=[(0, cut)], target=1, dtype=BF16, after=(one_high,))
+    one_low, one_high = part(coeff=coeff_all, spans=[(0, cut), (cut, occ)], target=1, dtype=BF16)
     near = sent(one_high, ahead)
     far_a = sent(back_a, back_on)
     summed = (chain.astype(wide) + one_low.astype(wide)).astype(BF16)
     last = sent(summed, ahead)
     far_b = sent(back_b, back_on)
-    (out,) = part(coeff=coeff_all, spans=[(0, occ)], target=0, dtype=wide, after=(back_a,))
+    (out,) = part(coeff=coeff_all, spans=[(0, occ)], target=0, dtype=wide, after=(back_b,))
     added = jnp.concatenate([last.astype(wide), near[: half - cut].astype(wide) + far_a.astype(wide), near[half - cut :].astype(wide) + far_b.astype(wide)])
     return out + added
 

time: 72.8 us -> 73.9 us (1.015)
  waiting for transfers between devices: 22.7 us -> 28.3 us
  Pallas kernels: 23.7 us -> 19.9 us
    ppermute x7, waiting for transfers between devices: 19.2 us -> 24.7 us  [sent(): return lax.ppermute(array, 'task', route)]
    pallas_call x4 -> x3, Pallas kernels: 21.9 us -> 18.1 us  [partial_sum(): pl.pallas_call(functools.partial(partial_kernel, ids=ids, pieces=pieces,...]
  transfers between devices with their start and end apart: 14 -> 14, of which waited for: 7 -> 7; matrix products, arithmetic and copies ran while one was open for 2% -> 2% of each run, Pallas kernels for 25% -> 20%
where the time goes in v1:
time: 73.9 us; the launch traced here: 73.5 us
  waiting for transfers between devices  28.3 us (38%)
  starting transfers between devices  20.2 us (27%)
  Pallas kernels  19.9 us (27%)
  other arithmetic  3.15 us (4%)
  local copies, waits for them, and re-layouts  1.14 us (2%)
  between operations  0.79 us (1%)
    ppermute x7, waiting for transfers between devices, sent(): return lax.ppermute(array, 'task', route)  24.7 us
    pallas_call x3, Pallas kernels, partial_sum(): pl.pallas_call(functools.partial(partial_kernel, ids=ids, pieces=pieces,...  18.1 us
    ppermute x7, starting transfers between devices, sent(): return lax.ppermute(array, 'task', route)  12.3 us
    ppermute x4, starting transfers between devices, local(): lax.ppermute(block, 'occ', [(r ^ 1, r) for r in range(ranks)])  4.85 us
    ppermute x3, starting transfers between devices, local(): lax.ppermute(rows, 'occ', [((r + 2 * d) % ranks, r) for r in range(ranks)])  3.11 us
    ppermute x3, waiting for transfers between devices, local(): lax.ppermute(rows, 'occ', [((r + 2 * d) % ranks, r) for r in range(ranks)])  2.61 us
    pallas_call x1, Pallas kernels, lists_of(): pl.pallas_call(functools.partial(list_kernel, stride=stride, zero_block=n...  1.8 us
    add x1, other arithmetic, local(): return out + added  1.79 us
  transfers between devices with their start and end apart: 14, of which 7 were waited for; matrix products, arithmetic and copies ran while one was open for 2% of the time, Pallas kernels for 20%

profile of v1, /device:TPU:1, one launch (start us, length us, event | category | flops | bytes accessed | tf_op | source)
XLA Modules:
  0.0 73.5 jit_solution(690929903643210744)
XLA Ops:
  0.0 3.2 %collective-permute-start.3 = (bf16[25,1536]{1,0:T(8,128)(2,1)}, bf16[25,1536]{1,0:T(8,128)(2,1)S(1)}, u32[]{:S(2)}, u32[]{:S(2)}) collective-permute-start(bf16[25,1536]{1,0:T(8,128)(2,1)} %bitcast.1), channel_id=1, source_target_pairs={{1,0},{0,1},{3,2},{2,3},{5,4},{4,5},{7,6},{6,7},{9,8},{8,9},{11,10... | collective-permute-start | bytes 230408 | tf_op jit(solution)/shard_map/ppermute | solution.py:286
  3.2 0.0 collective-permute-start.2
  3.2 2.0 %collective-permute-start.1 = (bf16[25,1536]{1,0:T(8,128)(2,1)}, bf16[25,1536]{1,0:T(8,128)(2,1)S(1)}, u32[]{:S(2)}, u32[]{:S(2)}) collective-permute-start(bf16[25,1536]{1,0:T(8,128)(2,1)} %bitcast.3), channel_id=1, source_target_pairs={{4,0},{5,1},{6,2},{7,3},{0,4},{1,5},{2,6},{3,7},{12,8},{13,9},{14,... | collective-permute-start | bytes 230408 | tf_op jit(solution)/shard_map/ppermute | solution.py:281
  5.2 1.2 %collective-permute-start = (bf16[25,1536]{1,0:T(8,128)(2,1)}, bf16[25,1536]{1,0:T(8,128)(2,1)S(1)}, u32[]{:S(2)}, u32[]{:S(2)}) collective-permute-start(bf16[25,1536]{1,0:T(8,128)(2,1)} %bitcast.4), channel_id=1, source_target_pairs={{2,0},{3,1},{4,2},{5,3},{6,4},{7,5},{0,6},{1,7},{10,8},{11,9},{12,... | collective-permute-start | bytes 230408 | tf_op jit(solution)/shard_map/ppermute | solution.py:281
  7.0 1.8 %lists.1.lists_ref = s32[1515]{0:T(1024)} custom-call(s32[160]{0:T(256)} %mu_ref.1, s32[160]{0:T(256)} %nu_ref.1, s32[160]{0:T(256)} %live_ref.1, s32[20]{0:T(128)} %target_ref.1, s32[1]{0:T(128)S(6)} %copy.8.count_ref), custom_call_target="tpu_custom_call" | custom-call | flops 2000000000 | bytes 10000 | tf_op jit(solution)/shard_map/lists/pallas_call | solution.py:222
  8.8 2.3 %collective-permute-done.2.refs_6_ = bf16[25,1536]{1,0:T(8,128)(2,1)S(1)} collective-permute-done((bf16[25,1536]{1,0:T(8,128)(2,1)}, bf16[25,1536]{1,0:T(8,128)(2,1)S(1)}, u32[]{:S(2)}, u32[]{:S(2)}) %collective-permute-start.2) | collective-permute-done | bytes 76832 | tf_op jit(solution)/shard_map/ppermute | solution.py:281
  11.1 0.0 copy-start.4
  11.1 0.0 collective-permute-done.1.refs_4_
  11.1 0.0 copy-start.5
  11.1 0.3 collective-permute-done.refs_2_
  11.4 0.0 copy-start.6
  11.4 1.1 %collective-permute-start.4 = (bf16[25,1536]{1,0:T(8,128)(2,1)S(1)}, bf16[25,1536]{1,0:T(8,128)(2,1)S(1)}, u32[]{:S(2)}, u32[]{:S(2)}) collective-permute-start(bf16[25,1536]{1,0:T(8,128)(2,1)S(1)} %collective-permute-done.refs_2_), channel_id=1, source_target_pairs={{1,0},{0,1},{3,2},{2,3},{5,4},{4,5},{7,6},{6,7},{9,8},{8,9},{11,10... | collective-permute-start | bytes 230408 | tf_op jit(solution)/shard_map/ppermute | solution.py:286
  12.5 0.0 collective-permute-start.5
  12.5 0.5 collective-permute-start.6
  13.0 0.0 collective-permute-done.3.refs_1_
  13.0 0.0 copy-start.3
  13.0 0.4 collective-permute-done.4.refs_3_
  13.5 0.0 copy-start.7
  13.5 0.4 collective-permute-done.5.refs_5_
  13.8 0.0 copy-start.8
  13.8 0.2 collective-permute-done.6.refs_7_
  14.0 0.0 copy-done.4
  14.0 0.0 copy-done.5
  14.0 0.0 copy-done.6
  14.0 0.0 copy-done.3
  14.0 0.1 copy-done.7
  14.1 0.4 copy-done.8
  14.5 0.0 copy-start.9
  14.5 0.6 copy-done.9
  15.1 5.5 %partial.3 = (bf16[1568,256]{1,0:T(8,128)(2,1)}, bf16[8,200,128]{2,1,0:T(8,128)(2,1)}, bf16[11,200,128]{2,1,0:T(8,128)(2,1)}, bf16[6,200,128]{2,1,0:T(8,128)(2,1)}) custom-call(s32[1515]{0:T(1024)} %lists.1.lists_ref, bf16[160,8,32,128]{3,2,1,0:T(8,128)(2,1)} %tiles_ref.5, bf16[25,1536]{1,0:T(8,128)(2,1)} %bitcast.5, bf16[25,1536]{1,0:T(8,128)(2,1)} %bitcast.6, ...), custom_call_target="tpu_custom_call" | custom-call | flops 6000000000 | bytes 10000000 | tf_op jit(solution)/shard_map/partial/pallas_call | solution.py:259
  20.6 1.6 %collective-permute-start.7 = (bf16[6,200,128]{2,1,0:T(8,128)(2,1)}, bf16[6,200,128]{2,1,0:T(8,128)(2,1)S(1)}, u32[]{:S(2)}, u32[]{:S(2)}) collective-permute-start(bf16[6,200,128]{2,1,0:T(8,128)(2,1)} %get-tuple-element.20), channel_id=1, source_target_pairs={{0,24},{8,0},{16,8},{24,16},{32,56},{40,32},{48,40},{56,48},{64,88... | collective-permute-start | bytes 921608 | tf_op jit(solution)/shard_map/ppermute | solution.py:299
  22.2 4.9 %collective-permute-start.8 = (bf16[8,200,128]{2,1,0:T(8,128)(2,1)}, bf16[8,200,128]{2,1,0:T(8,128)(2,1)S(1)}, u32[]{:S(2)}, u32[]{:S(2)}) collective-permute-start(bf16[8,200,128]{2,1,0:T(8,128)(2,1)} %get-tuple-element.21), channel_id=1, source_target_pairs={{0,8},{8,16},{16,24},{24,32},{32,40},{40,48},{48,56},{56,64},{64,7... | collective-permute-start | bytes 1228808 | tf_op jit(solution)/shard_map/ppermute | solution.py:299
  27.1 4.3 %collective-permute-start.11 = (bf16[11,200,128]{2,1,0:T(8,128)(2,1)}, bf16[11,200,128]{2,1,0:T(8,128)(2,1)S(1)}, u32[]{:S(2)}, u32[]{:S(2)}) collective-permute-start(bf16[11,200,128]{2,1,0:T(8,128)(2,1)} %get-tuple-element.24), channel_id=1, source_target_pairs={{0,24},{8,0},{16,8},{24,16},{32,56},{40,32},{48,40},{56,48},{64,88... | collective-permute-start | bytes 1689608 | tf_op jit(solution)/shard_map/ppermute | solution.py:299
  31.4 0.0 copy-start
  31.4 0.0 copy-start.1
  31.4 0.0 copy-start.2
  31.4 7.6 %partial.5 = (bf16[8,200,128]{2,1,0:T(8,128)(2,1)}, bf16[17,200,128]{2,1,0:T(8,128)(2,1)}) custom-call(s32[1515]{0:T(1024)} %lists.1.lists_ref, bf16[160,8,32,128]{3,2,1,0:T(8,128)(2,1)} %tiles_ref.5, bf16[25,1536]{1,0:T(8,128)(2,1)} %bitcast.7, bf16[1568,256]{1,0:T(8,128)(2,1)} %get-tuple-element.19.refs_0_), custom_call_target="tpu_custom_call" | custom-call | flops 6000000000 | bytes 10000000 | tf_op jit(solution)/shard_map/partial/pallas_call | solution.py:259
  39.1 0.1 collective-permute-start.10
  39.2 0.0 collective-permute-done.7.refs_1_
  39.2 0.1 collective-permute-start.13
  39.3 0.0 collective-permute-done.8
  39.3 1.1 %add_convert_fusion = bf16[8,200,128]{2,1,0:T(8,128)(2,1)S(1)} fusion(bf16[8,200,128]{2,1,0:T(8,128)(2,1)} %get-tuple-element.22, bf16[8,200,128]{2,1,0:T(8,128)(2,1)S(1)} %collective-permute-done.8), kind=kLoop, calls=%fused_computation.2 | loop fusion | flops 819200 | bytes 1228800 | tf_op jit(solution)/shard_map/convert_element_type | solution.py:308
  40.4 1.3 %collective-permute-start.9 = (bf16[8,200,128]{2,1,0:T(8,128)(2,1)S(1)}, bf16[8,200,128]{2,1,0:T(8,128)(2,1)S(1)}, u32[]{:S(2)}, u32[]{:S(2)}) collective-permute-start(bf16[8,200,128]{2,1,0:T(8,128)(2,1)S(1)} %add_convert_fusion), channel_id=1, source_target_pairs={{0,8},{8,16},{16,24},{24,32},{32,40},{40,48},{48,56},{56,64},{64,7... | collective-permute-start | bytes 1228808 | tf_op jit(solution)/shard_map/ppermute | solution.py:299
  41.7 11.7 %collective-permute-done.11 = bf16[11,200,128]{2,1,0:T(8,128)(2,1)S(1)} collective-permute-done((bf16[11,200,128]{2,1,0:T(8,128)(2,1)}, bf16[11,200,128]{2,1,0:T(8,128)(2,1)S(1)}, u32[]{:S(2)}, u32[]{:S(2)}) %collective-permute-start.11) | collective-permute-done | bytes 563232 | tf_op jit(solution)/shard_map/ppermute | solution.py:299
  53.4 0.0 collective-permute-start.12
  53.4 0.0 copy-done
  53.4 0.0 copy-done.1
  53.4 0.0 copy-done.2
  53.4 5.0 %partial.4 = f32[25,200,128]{2,1,0:T(8,128)S(1)} custom-call(s32[1515]{0:T(1024)S(1)} %copy-done.2, bf16[160,8,32,128]{3,2,1,0:T(8,128)(2,1)} %tiles_ref.5, bf16[25,1536]{1,0:T(8,128)(2,1)S(1)} %bitcast.8, bf16[1568,256]{1,0:T(8,128)(2,1)S(1)} %copy-done.1, bf16[6,200,128]{2,1,0:T(8,128)(2,1)S(1)} %collective-permute-done.7.refs_1_), custom_call_target="tpu_custom_call" | custom-call | flops 6000000000 | bytes 10000000 | tf_op jit(solution)/shard_map/partial/pallas_call | solution.py:259
  58.4 13.0 %collective-permute-done.9 = bf16[8,200,128]{2,1,0:T(8,128)(2,1)S(1)} collective-permute-done((bf16[8,200,128]{2,1,0:T(8,128)(2,1)S(1)}, bf16[8,200,128]{2,1,0:T(8,128)(2,1)S(1)}, u32[]{:S(2)}, u32[]{:S(2)}) %collective-permute-start.9) | collective-permute-done | bytes 409632 | tf_op jit(solution)/shard_map/ppermute | solution.py:299
  71.4 0.1 convert_element_type.27
  71.5 0.0 collective-permute-done.13
  71.5 0.0 collective-permute-done.10
  71.5 0.1 convert_add_fusion.1
  71.6 0.0 collective-permute-done.12
  71.6 0.1 convert_add_fusion
  71.7 1.8 %maximum_add_fusion = f32[25,200,128]{2,1,0:T(8,128)} fusion(f32[25,200,128]{2,1,0:T(8,128)S(1)} %partial.4, f32[6,200,128]{2,1,0:T(8,128)S(1)} %convert_add_fusion.1, f32[11,200,128]{2,1,0:T(8,128)S(1)} %convert_add_fusion, f32[8,200,128]{2,1,0:T(8,128)S(1)} %convert_element_type.27), kind=kLoop, calls=%fused_computation | loop fusion | flops 1920000 | bytes 7680000 | tf_op jit(solution)/shard_map/add | solution.py:313
Async XLA Ops:
  0.0 13.0 %collective-permute-start.3 = (bf16[25,1536]{1,0:T(8,128)(2,1)}, bf16[25,1536]{1,0:T(8,128)(2,1)S(1)}, u32[]{:S(2)}, u32[]{:S(2)}) collective-permute-start(bf16[25,1536]{1,0:T(8,128)(2,1)} %bitcast.1), channel_id=1, source_target_pairs={{1,0},{0,1},{3,2},{2,3},{5,4},{4,5},{7,6},{6,7},{9,8},{8,9},{11,10... | collective-permute-start | bytes 230408 | tf_op jit(solution)/shard_map/ppermute | solution.py:286
  3.2 7.9 %collective-permute-start.2 = (bf16[25,1536]{1,0:T(8,128)(2,1)}, bf16[25,1536]{1,0:T(8,128)(2,1)S(1)}, u32[]{:S(2)}, u32[]{:S(2)}) collective-permute-start(bf16[25,1536]{1,0:T(8,128)(2,1)} %bitcast.2), channel_id=1, source_target_pairs={{6,0},{7,1},{0,2},{1,3},{2,4},{3,5},{4,6},{5,7},{14,8},{15,9},{8,1... | collective-permute-start | bytes 230408 | tf_op jit(solution)/shard_map/ppermute | solution.py:281
  3.2 7.9 %collective-permute-start.1 = (bf16[25,1536]{1,0:T(8,128)(2,1)}, bf16[25,1536]{1,0:T(8,128)(2,1)S(1)}, u32[]{:S(2)}, u32[]{:S(2)}) collective-permute-start(bf16[25,1536]{1,0:T(8,128)(2,1)} %bitcast.3), channel_id=1, source_target_pairs={{4,0},{5,1},{6,2},{7,3},{0,4},{1,5},{2,6},{3,7},{12,8},{13,9},{14,... | collective-permute-start | bytes 230408 | tf_op jit(solution)/shard_map/ppermute | solution.py:281
  5.2 6.2 %collective-permute-start = (bf16[25,1536]{1,0:T(8,128)(2,1)}, bf16[25,1536]{1,0:T(8,128)(2,1)S(1)}, u32[]{:S(2)}, u32[]{:S(2)}) collective-permute-start(bf16[25,1536]{1,0:T(8,128)(2,1)} %bitcast.4), channel_id=1, source_target_pairs={{2,0},{3,1},{4,2},{5,3},{6,4},{7,5},{0,6},{1,7},{10,8},{11,9},{12,... | collective-permute-start | bytes 230408 | tf_op jit(solution)/shard_map/ppermute | solution.py:281
  11.1 2.9 %copy-start.4 = (bf16[25,1536]{1,0:T(8,128)(2,1)}, bf16[25,1536]{1,0:T(8,128)(2,1)S(1)}, u32[]{:S(2)}) copy-start(bf16[25,1536]{1,0:T(8,128)(2,1)S(1)} %collective-permute-done.2.refs_6_) | copy-start | bytes 230404
  11.1 2.9 %copy-start.5 = (bf16[25,1536]{1,0:T(8,128)(2,1)}, bf16[25,1536]{1,0:T(8,128)(2,1)S(1)}, u32[]{:S(2)}) copy-start(bf16[25,1536]{1,0:T(8,128)(2,1)S(1)} %collective-permute-done.1.refs_4_) | copy-start | bytes 230404
  11.4 2.6 %copy-start.6 = (bf16[25,1536]{1,0:T(8,128)(2,1)}, bf16[25,1536]{1,0:T(8,128)(2,1)S(1)}, u32[]{:S(2)}) copy-start(bf16[25,1536]{1,0:T(8,128)(2,1)S(1)} %collective-permute-done.refs_2_) | copy-start | bytes 230404
  11.4 2.1 %collective-permute-start.4 = (bf16[25,1536]{1,0:T(8,128)(2,1)S(1)}, bf16[25,1536]{1,0:T(8,128)(2,1)S(1)}, u32[]{:S(2)}, u32[]{:S(2)}) collective-permute-start(bf16[25,1536]{1,0:T(8,128)(2,1)S(1)} %collective-permute-done.refs_2_), channel_id=1, source_target_pairs={{1,0},{0,1},{3,2},{2,3},{5,4},{4,5},{7,6},{6,7},{9,8},{8,9},{11,10... | collective-permute-start | bytes 230408 | tf_op jit(solution)/shard_map/ppermute | solution.py:286
  12.5 1.3 %collective-permute-start.5 = (bf16[25,1536]{1,0:T(8,128)(2,1)S(1)}, bf16[25,1536]{1,0:T(8,128)(2,1)S(1)}, u32[]{:S(2)}, u32[]{:S(2)}) collective-permute-start(bf16[25,1536]{1,0:T(8,128)(2,1)S(1)} %collective-permute-done.1.refs_4_), channel_id=1, source_target_pairs={{1,0},{0,1},{3,2},{2,3},{5,4},{4,5},{7,6},{6,7},{9,8},{8,9},{11,10... | collective-permute-start | bytes 230408 | tf_op jit(solution)/shard_map/ppermute | solution.py:286
  12.5 1.5 %collective-permute-start.6 = (bf16[25,1536]{1,0:T(8,128)(2,1)S(1)}, bf16[25,1536]{1,0:T(8,128)(2,1)S(1)}, u32[]{:S(2)}, u32[]{:S(2)}) collective-permute-start(bf16[25,1536]{1,0:T(8,128)(2,1)S(1)} %collective-permute-done.2.refs_6_), channel_id=1, source_target_pairs={{1,0},{0,1},{3,2},{2,3},{5,4},{4,5},{7,6},{6,7},{9,8},{8,9},{11,10... | collective-permute-start | bytes 230408 | tf_op jit(solution)/shard_map/ppermute | solution.py:286
  13.0 1.0 %copy-start.3 = (bf16[25,1536]{1,0:T(8,128)(2,1)}, bf16[25,1536]{1,0:T(8,128)(2,1)S(1)}, u32[]{:S(2)}) copy-start(bf16[25,1536]{1,0:T(8,128)(2,1)S(1)} %collective-permute-done.3.refs_1_) | copy-start | bytes 230404
  13.5 0.6 copy-start.7
  13.8 0.6 copy-start.8
  14.5 0.6 copy-start.9
  20.6 18.6 %collective-permute-start.7 = (bf16[6,200,128]{2,1,0:T(8,128)(2,1)}, bf16[6,200,128]{2,1,0:T(8,128)(2,1)S(1)}, u32[]{:S(2)}, u32[]{:S(2)}) collective-permute-start(bf16[6,200,128]{2,1,0:T(8,128)(2,1)} %get-tuple-element.20), channel_id=1, source_target_pairs={{0,24},{8,0},{16,8},{24,16},{32,56},{40,32},{48,40},{56,48},{64,88... | collective-permute-start | bytes 921608 | tf_op jit(solution)/shard_map/ppermute | solution.py:299
  22.2 17.1 %collective-permute-start.8 = (bf16[8,200,128]{2,1,0:T(8,128)(2,1)}, bf16[8,200,128]{2,1,0:T(8,128)(2,1)S(1)}, u32[]{:S(2)}, u32[]{:S(2)}) collective-permute-start(bf16[8,200,128]{2,1,0:T(8,128)(2,1)} %get-tuple-element.21), channel_id=1, source_target_pairs={{0,8},{8,16},{16,24},{24,32},{32,40},{40,48},{48,56},{56,64},{64,7... | collective-permute-start | bytes 1228808 | tf_op jit(solution)/shard_map/ppermute | solution.py:299
  27.1 26.3 %collective-permute-start.11 = (bf16[11,200,128]{2,1,0:T(8,128)(2,1)}, bf16[11,200,128]{2,1,0:T(8,128)(2,1)S(1)}, u32[]{:S(2)}, u32[]{:S(2)}) collective-permute-start(bf16[11,200,128]{2,1,0:T(8,128)(2,1)} %get-tuple-element.24), channel_id=1, source_target_pairs={{0,24},{8,0},{16,8},{24,16},{32,56},{40,32},{48,40},{56,48},{64,88... | collective-permute-start | bytes 1689608 | tf_op jit(solution)/shard_map/ppermute | solution.py:299
  31.4 21.9 %copy-start = (bf16[1536,25]{0,1:T(8,128)(2,1)S(1)}, bf16[1536,25]{0,1:T(8,128)(2,1)}, u32[]{:S(2)}) copy-start(bf16[1536,25]{0,1:T(8,128)(2,1)} %param.8) | copy-start | bytes 230404
  31.4 21.9 %copy-start.1 = (bf16[1568,256]{1,0:T(8,128)(2,1)S(1)}, bf16[1568,256]{1,0:T(8,128)(2,1)}, u32[]{:S(2)}) copy-start(bf16[1568,256]{1,0:T(8,128)(2,1)} %get-tuple-element.19.refs_0_) | copy-start | bytes 2408452
  31.4 21.9 %copy-start.2 = (s32[1515]{0:T(1024)S(1)}, s32[1515]{0:T(1024)}, u32[]{:S(2)}) copy-start(s32[1515]{0:T(1024)} %lists.1.lists_ref) | copy-start | bytes 18184
  39.1 32.4 %collective-permute-start.10 = (bf16[17,200,128]{2,1,0:T(8,128)(2,1)}, bf16[17,200,128]{2,1,0:T(8,128)(2,1)S(1)}, u32[]{:S(2)}, u32[]{:S(2)}) collective-permute-start(bf16[17,200,128]{2,1,0:T(8,128)(2,1)} %get-tuple-element.23), channel_id=1, source_target_pairs={{0,8},{8,16},{16,24},{24,32},{32,40},{40,48},{48,56},{56,64},{64,7... | collective-permute-start | bytes 2611208 | tf_op jit(solution)/shard_map/ppermute | solution.py:299
  39.2 32.3 %collective-permute-start.13 = (bf16[6,200,128]{2,1,0:T(8,128)(2,1)S(1)}, bf16[6,200,128]{2,1,0:T(8,128)(2,1)S(1)}, u32[]{:S(2)}, u32[]{:S(2)}) collective-permute-start(bf16[6,200,128]{2,1,0:T(8,128)(2,1)S(1)} %collective-permute-done.7.refs_1_), channel_id=1, source_target_pairs={{24,16},{0,24},{8,32},{16,40},{56,48},{32,56},{40,64},{48,72},{88,... | collective-permute-start | bytes 921608 | tf_op jit(solution)/shard_map/ppermute | solution.py:299
  40.4 31.0 %collective-permute-start.9 = (bf16[8,200,128]{2,1,0:T(8,128)(2,1)S(1)}, bf16[8,200,128]{2,1,0:T(8,128)(2,1)S(1)}, u32[]{:S(2)}, u32[]{:S(2)}) collective-permute-start(bf16[8,200,128]{2,1,0:T(8,128)(2,1)S(1)} %add_convert_fusion), channel_id=1, source_target_pairs={{0,8},{8,16},{16,24},{24,32},{32,40},{40,48},{48,56},{56,64},{64,7... | collective-permute-start | bytes 1228808 | tf_op jit(solution)/shard_map/ppermute | solution.py:299
  53.4 18.2 %collective-permute-start.12 = (bf16[11,200,128]{2,1,0:T(8,128)(2,1)S(1)}, bf16[11,200,128]{2,1,0:T(8,128)(2,1)S(1)}, u32[]{:S(2)}, u32[]{:S(2)}) collective-permute-start(bf16[11,200,128]{2,1,0:T(8,128)(2,1)S(1)} %collective-permute-done.11), channel_id=1, source_target_pairs={{24,16},{0,24},{8,32},{16,40},{56,48},{32,56},{40,64},{48,72},{88,... | collective-permute-start | bytes 1689608 | tf_op jit(solution)/shard_map/ppermute | solution.py:299
